TPU v7x, 32 devices: a whole 2x2x4 slice. The times are simulated.
32 devices in a mesh: dp: 8 (over y, x, core), tensor: 4 (over z).
Axes of the slice: x: 2, y: 2, z: 4, core: 2. Of those that a mesh axis runs over, the one named last changes fastest.
Arguments:
- layer_input: bfloat16 [16384, 4096], P('dp', 'tensor'), may hold values from -54 to 54
- queries: bfloat16 [16384, 2048], P('dp', 'tensor'), may hold values from -6 to 6
- keys_values: bfloat16 [16384, 2, 1024], P('dp', None, 'tensor'), may hold values from -6 to 6
- out_grads: bfloat16 [16384, 2048], P('dp', 'tensor'), may hold values from -6 to 6
- log_sums: bfloat16 [16384, 16], P('dp', 'tensor'), may hold values from 2.5 to 5.5
- deltas: bfloat16 [16384, 16], P('dp', 'tensor'), may hold values from -1.5 to 1.5
- tile_fill: int32 [8, 16], replicated, may hold values from 1 to 128, as said below
- tile_cont: int32 [8, 16], replicated, may hold values from 0 to 1, as said below
- moment_first: float32 [4096, 2, 1024], P(('tensor', 'dp')), may hold values from -2 to 2
- moment_second: float32 [2, 8], replicated, may hold values from 0.05 to 0.5
Outputs:
- update: float32 [4096, 2, 1024], P(('tensor', 'dp'))
- new_first: float32 [4096, 2, 1024], P(('tensor', 'dp'))
- new_second: float32 [2, 8], replicated
Inputs may be any that keep to these rules, and one draw needn't show every extreme that they name: `tile_fill`: a tile followed by a tile with tile_cont 1 has all 128 positions live. Documents span one or two tiles: tile_cont is 0 for the first tile of each group and never 1 for two tiles in a row.
All inputs are finite; a program needn't handle non-finite values.
Results may differ from a plain program's by a relative error of at most 0.0055.
Values may be sent and summed in bfloat16 or wider, within the bound.
A program may use at most 64 MiB of HBM per device.

v0:
```python
import functools
import math

import jax
import jax.numpy as jnp
from jax import lax
from jax.experimental import pallas as pl
from jax.experimental.pallas import tpu as pltpu
from jax.sharding import PartitionSpec as P

D = 4096
HD = 128

ADAM_ONE = 0.9
ADAM_TWO = 0.95
ADAM_EPS = 1e-08
MESH = pl.DeviceIdType.MESH
NT = (((1,), (1,)), ((), ()))


def attend_kernel(tiles, group_size, fill_ref, cont_ref, q_ref, k_ref, v_ref, do_ref, lse_ref, delta_ref, out_ref):
    group = lax.axis_index("dp")
    block = k_ref.shape[0] // tiles
    scale_qk = HD ** (-0.5)
    wide = 2 * group_size * block
    key_place = lax.broadcasted_iota(jnp.int32, (block, wide), 0)
    column = lax.broadcasted_iota(jnp.int32, (block, wide), 1)
    query_place = column % block
    is_next = column >= group_size * block

    def one_tile(tile, carry):
        after = jnp.minimum(tile + 1, tiles - 1)
        here = pl.ds(pl.multiple_of(tile * block, block), block)
        there = pl.ds(pl.multiple_of(after * block, block), block)
        fill_here = fill_ref[group, tile]
        fill_there = jnp.where(tile + 1 < tiles, fill_ref[group, after] * (cont_ref[group, after] == 1).astype(jnp.int32), 0)
        heads = [slice(h * HD, (h + 1) * HD) for h in range(group_size)]
        q_cat = jnp.concatenate([q_ref[w, h] for w in (here, there) for h in heads], 0)
        do_cat = jnp.concatenate([do_ref[w, h] for w in (here, there) for h in heads], 0)
        lse = jnp.concatenate([lse_ref[0, h : h + 1, w] for w in (here, there) for h in range(group_size)], 1)
        delta = jnp.concatenate([delta_ref[0, h : h + 1, w] for w in (here, there) for h in range(group_size)], 1)
        scores = lax.dot_general(k_ref[here, :], q_cat, NT, preferred_element_type=jnp.float32) * scale_qk
        limit = jnp.where(is_next, fill_there, fill_here)
        allowed = (query_place < limit) & (is_next | (query_place >= key_place))
        prob = jnp.where(allowed, jnp.exp(scores - lse), 0.0)
        dprob = lax.dot_general(v_ref[here, :], do_cat, NT, preferred_element_type=jnp.float32)
        dscore = prob * (dprob - delta)
        value_grad = jnp.dot(prob.astype(jnp.bfloat16), do_cat, preferred_element_type=jnp.float32)
        key_grad = jnp.dot(dscore.astype(jnp.bfloat16), q_cat, preferred_element_type=jnp.float32) * scale_qk
        out_ref[0, here, :] = key_grad.astype(jnp.bfloat16)
        out_ref[1, here, :] = value_grad.astype(jnp.bfloat16)
        return carry

    lax.fori_loop(0, tiles, one_tile, 0, unroll=2)


def attend(queries, keys, values, out_grads, lse_rows, delta_rows, tile_fill, tile_cont):
    tokens = queries.shape[0]
    kv_local = keys.shape[1] // HD
    group_size = queries.shape[1] // keys.shape[1]
    tiles = tile_fill.shape[1]
    smem = pl.BlockSpec(memory_space=pltpu.SMEM)
    q_spec = pl.BlockSpec((tokens, group_size * HD), lambda h: (0, h))
    k_spec = pl.BlockSpec((tokens, HD), lambda h: (0, h))
    row_spec = pl.BlockSpec((1, group_size, tokens), lambda h: (h, 0, 0))
    return pl.pallas_call(
        functools.partial(attend_kernel, tiles, group_size),
        grid=(kv_local,),
        out_shape=jax.ShapeDtypeStruct((2 * kv_local, tokens, HD), jnp.bfloat16),
        in_specs=[smem, smem, q_spec, k_spec, k_spec, q_spec, row_spec, row_spec],
        out_specs=pl.BlockSpec((2, tokens, HD), lambda h: (h, 0, 0)),
        compiler_params=pltpu.CompilerParams(vmem_limit_bytes=32 * 2**20),
    )(tile_fill, tile_cont, queries, keys, values, out_grads, lse_rows, delta_rows)


def sum_kernel(
    groups, planes, inv, kv_ref, layer_ref, out_ref, sq_ref,
    layer, flipped, gathered, terms, pair_send, pair_recv, chip_send, chip_recv, sq_groups, sq_mid, sq_planes,
    load_sem, kv_right, kv_left, kv_recv, pair_ssem, pair_rsem, chip_ssem, chip_rsem,
    sqg_ssem, sqg_rsem, sqp_ssem, sqp_rsem,
):
    me, plane = lax.axis_index("dp"), lax.axis_index("tensor")
    chips = groups // 2
    chip, core = me // 2, me % 2
    partner = me + 1 - 2 * core
    chunks, tokens, _ = kv_ref.shape
    rows = layer_ref.shape[1]
    rows_out = rows // groups

    load = pltpu.make_async_copy(layer_ref, layer, load_sem)
    load.start()

    barrier = pltpu.get_barrier_semaphore()
    for step in range(1, groups):
        pl.semaphore_signal(barrier, inc=1, device_id=(lax.rem(me + step, groups), plane), device_id_type=MESH)
    for step in range(1, planes):
        pl.semaphore_signal(barrier, inc=1, device_id=(me, lax.rem(plane + step, planes)), device_id_type=MESH)
    pl.semaphore_wait(barrier, groups + planes - 2)

    def to_right(source, c, p):
        return pltpu.make_async_remote_copy(
            src_ref=source, dst_ref=gathered.at[c, p], send_sem=kv_right.at[c, p], recv_sem=kv_recv.at[c, p],
            device_id=(me, jnp.minimum(plane + 1, planes - 1)), device_id_type=MESH,
        )

    def to_left(source, c, p):
        return pltpu.make_async_remote_copy(
            src_ref=source, dst_ref=gathered.at[c, p], send_sem=kv_left.at[c, p], recv_sem=kv_recv.at[c, p],
            device_id=(me, jnp.maximum(plane - 1, 0)), device_id_type=MESH,
        )

    def send_own(c):
        @pl.when(plane < planes - 1)
        def _():
            to_right(kv_ref.at[c], c, plane).start()

        @pl.when(plane > 0)
        def _():
            to_left(kv_ref.at[c], c, plane).start()

    row_block = min(256, rows)

    def product(piece_ref, c, p):
        def one(i, carry):
            at = pl.ds(pl.multiple_of(i * row_block, row_block), row_block)
            terms[c, p, at, :] = jnp.dot(flipped[at, :], piece_ref[...], preferred_element_type=jnp.float32)
            return carry

        lax.fori_loop(0, rows // row_block, one, 0)

    def slice_of(k, parity):
        return pl.ds(pl.multiple_of((2 * k + parity) * rows_out, rows_out), rows_out)

    def pair_copy(c):
        return pltpu.make_async_remote_copy(
            src_ref=pair_send.at[c], dst_ref=pair_recv.at[c], send_sem=pair_ssem.at[c], recv_sem=pair_rsem.at[c],
            device_id=(partner, plane), device_id_type=MESH,
        )

    def chip_copy(c, step):
        other = lax.rem(chip + step, chips)
        return pltpu.make_async_remote_copy(
            src_ref=chip_send.at[c, step - 1], dst_ref=chip_recv.at[c, step - 1],
            send_sem=chip_ssem.at[c, step - 1], recv_sem=chip_rsem.at[c, step - 1],
            device_id=(2 * other + core, plane), device_id_type=MESH,
        )

    def stage_one(c):
        for k in range(chips):
            pair_send[c, k] = terms[c, :, slice_of(k, 1 - core), :].astype(jnp.bfloat16)
        pair_copy(c).start()

    def stage_two(c):
        pair_copy(c).wait_recv()
        for step in range(1, chips):
            other = lax.rem(chip + step, chips)
            both = terms[c, :, slice_of(other, core), :] + pair_recv[c, other].astype(jnp.float32)
            chip_send[c, step - 1] = both.astype(jnp.bfloat16)
            chip_copy(c, step).start()

    def stage_three(c):
        total = terms[c, :, slice_of(chip, core), :] + pair_recv[c, chip].astype(jnp.float32)
        for step in range(1, chips):
            chip_copy(c, step).wait_recv()
            total = total + chip_recv[c, step - 1].astype(jnp.float32)
        total = total * inv
        out_ref[c] = total
        squares = jnp.sum(total * total, axis=1)
        sq_groups[me, c] = squares

    send_own(0)
    load.wait()
    flip_block = min(128, rows)

    def flip(i, carry):
        at = pl.ds(pl.multiple_of(i * flip_block, flip_block), flip_block)
        flipped[at, :] = layer[:, at].T
        return carry

    lax.fori_loop(0, rows // flip_block, flip, 0)

    def one_chunk(c, carry):
        product(kv_ref.at[c], c, plane)
        for dist in range(1, planes):
            left, right = plane - dist, plane + dist

            @pl.when(left >= 0)
            def _():
                to_right(kv_ref.at[c], c, left).wait_recv()

                @pl.when(plane < planes - 1)
                def _():
                    to_right(gathered.at[c, left], c, left).start()

            @pl.when(right < planes)
            def _():
                to_left(kv_ref.at[c], c, right).wait_recv()

                @pl.when(plane > 0)
                def _():
                    to_left(gathered.at[c, right], c, right).start()

            if dist == 1:
                @pl.when(c + 1 < chunks)
                def _():
                    send_own(c + 1)

            @pl.when(left >= 0)
            def _():
                product(gathered.at[c, left], c, left)

            @pl.when(right < planes)
            def _():
                product(gathered.at[c, right], c, right)

            if dist == 1:
                @pl.when(c > 0)
                def _():
                    stage_two(c - 1)

            if dist == min(2, planes - 1):
                @pl.when(c > 0)
                def _():
                    stage_three(c - 1)

        stage_one(c)
        return carry

    lax.fori_loop(0, chunks, one_chunk, 0)
    stage_two(chunks - 1)
    stage_three(chunks - 1)

    def sq_group_copy(step):
        return pltpu.make_async_remote_copy(
            src_ref=sq_groups.at[me], dst_ref=sq_groups.at[me], send_sem=sqg_ssem.at[step - 1],
            recv_sem=sqg_rsem.at[step - 1],
            device_id=(lax.rem(me + step, groups), plane), device_id_type=MESH,
        )

    for step in range(1, groups):
        sq_group_copy(step).start()
    for step in range(1, groups):
        sq_group_copy(step).wait_recv()
    sq_mid[...] = sq_groups[0]
    for g in range(1, groups):
        sq_mid[...] += sq_groups[g]
    sq_planes[plane] = sq_mid[...]

    def sq_plane_copy(step):
        return pltpu.make_async_remote_copy(
            src_ref=sq_mid, dst_ref=sq_planes.at[plane], send_sem=sqp_ssem.at[step - 1],
            recv_sem=sqp_rsem.at[step - 1],
            device_id=(me, lax.rem(plane + step, planes)), device_id_type=MESH,
        )

    for step in range(1, planes):
        sq_plane_copy(step).start()
    for step in range(1, planes):
        sq_plane_copy(step).wait_recv()
    summed = sq_planes[0]
    for p in range(1, planes):
        summed = summed + sq_planes[p]
    sq_ref[...] = summed

    for step in range(1, groups):
        sq_group_copy(step).wait_send()
    for step in range(1, planes):
        sq_plane_copy(step).wait_send()

    def drain(c, carry):
        pair_copy(c).wait_send()
        for step in range(1, chips):
            chip_copy(c, step).wait_send()
        for p in range(planes):
            @pl.when((plane < planes - 1) & (p <= plane))
            def _():
                to_right(kv_ref.at[c], c, p).wait_send()

            @pl.when((plane > 0) & (p >= plane))
            def _():
                to_left(kv_ref.at[c], c, p).wait_send()
        return carry

    lax.fori_loop(0, chunks, drain, 0)


def sum_over_groups(kv_chunks, layer_input, groups, planes):
    chunks, tokens, _ = kv_chunks.shape
    rows = layer_input.shape[1]
    rows_out = rows // groups
    chips = groups // 2
    half, full = jnp.bfloat16, jnp.float32
    dma = pltpu.SemaphoreType.DMA
    vmem = pl.BlockSpec(memory_space=pltpu.VMEM)
    return pl.pallas_call(
        functools.partial(sum_kernel, groups, planes, 1.0 / math.sqrt(tokens * groups)),
        out_shape=(
            jax.ShapeDtypeStruct((chunks, planes, rows_out, HD), full),
            jax.ShapeDtypeStruct((chunks, planes, HD), full),
        ),
        in_specs=[vmem, pl.BlockSpec(memory_space=pl.ANY)],
        out_specs=(vmem, vmem),
        scratch_shapes=[
            pltpu.VMEM((tokens, rows), half),
            pltpu.VMEM((rows, tokens), half),
            pltpu.VMEM((chunks, planes, tokens, HD), half),
            pltpu.VMEM((chunks, planes, rows, HD), full),
            pltpu.VMEM((chunks, chips, planes, rows_out, HD), half),
            pltpu.VMEM((chunks, chips, planes, rows_out, HD), half),
            pltpu.VMEM((chunks, chips - 1, planes, rows_out, HD), half),
            pltpu.VMEM((chunks, chips - 1, planes, rows_out, HD), half),
            pltpu.VMEM((groups, chunks, planes, HD), full),
            pltpu.VMEM((chunks, planes, HD), full),
            pltpu.VMEM((planes, chunks, planes, HD), full),
            dma,
            dma((chunks, planes)),
            dma((chunks, planes)),
            dma((chunks, planes)),
            dma((chunks,)),
            dma((chunks,)),
            dma((chunks, chips - 1)),
            dma((chunks, chips - 1)),
            dma((groups - 1,)),
            dma((groups - 1,)),
            dma((planes - 1,)),
            dma((planes - 1,)),
        ],
        compiler_params=pltpu.CompilerParams(
            collective_id=0, has_side_effects=True, vmem_limit_bytes=56 * 2**20
        ),
    )(kv_chunks, layer_input)


def per_device(
    layer_input, queries, keys_values, out_grads, log_sums, deltas, tile_fill, tile_cont, moment_first, moment_second
):
    groups, planes = lax.axis_size("dp"), lax.axis_size("tensor")
    keys, values = keys_values[:, 0], keys_values[:, 1]
    tokens = queries.shape[0]
    kv_local = keys.shape[1] // HD
    lse_rows = log_sums.astype(jnp.float32).T.reshape(kv_local, -1, tokens)
    delta_rows = deltas.astype(jnp.float32).T.reshape(kv_local, -1, tokens)
    kv_chunks = attend(queries, keys, values, out_grads, lse_rows, delta_rows, tile_fill, tile_cont)
    summed, lane_squares = sum_over_groups(kv_chunks, layer_input, groups, planes)
    rows_out = summed.shape[2]
    heads_kv = moment_second.shape[1]
    parts = summed.reshape(kv_local, 2, planes, rows_out, HD)
    proj_grads = parts.transpose(3, 1, 2, 0, 4).reshape(rows_out, 2, -1)
    squares = jnp.sum(lane_squares.reshape(kv_local, 2, planes, HD), 3).transpose(1, 2, 0).reshape(2, heads_kv)
    new_first = ADAM_ONE * moment_first + (1 - ADAM_ONE) * proj_grads
    new_second = ADAM_TWO * moment_second + (1 - ADAM_TWO) * squares / (D * HD)
    step_size = jnp.sqrt(new_second / (1 - ADAM_TWO**2)) + ADAM_EPS
    scaled = (new_first / (1 - ADAM_ONE**2)).reshape(rows_out, 2, heads_kv, -1)
    update = (scaled / step_size[None, :, :, None]).reshape(proj_grads.shape)
    return (update, new_first, new_second)


def solution(mesh):
    in_specs = (
        P("dp", "tensor"),
        P("dp", "tensor"),
        P("dp", None, "tensor"),
        P("dp", "tensor"),
        P("dp", "tensor"),
        P("dp", "tensor"),
        P(),
        P(),
        P(("tensor", "dp"), None, None),
        P(),
    )
    out_specs = (P(("tensor", "dp"), None, None), P(("tensor", "dp"), None, None), P())
    return jax.shard_map(
        per_device, mesh=mesh, in_specs=in_specs, out_specs=out_specs, check_vma=False
    )
```

profile of v0, /device:TPU:0, one launch (start us, length us, event | category | flops | bytes accessed | tf_op | source)
XLA Modules:
  0.0 192.8 jit_solution(15414848760976079674)
XLA Ops:
  0.6 5.6 %fusion = (bf16[2048,1,256]{2,1,0:T(2,128)(2,1)S(1)}, bf16[2048,1,256]{2,1,0:T(2,128)(2,1)S(1)}) fusion(bf16[2048,2,256]{2,1,0:T(2,128)(2,1)} %param.12), kind=kLoop, calls=%fused_computation.12 | loop fusion | bytes 4194304 | tf_op jit(solution)/shard_map/slice | solution.py:338
  6.2 0.0 copy-start.6
  6.2 0.0 copy-start.7
  6.2 0.0 copy-start.3
  6.2 0.0 copy-start.4
  6.2 0.5 copy_bitcast_fusion
  6.7 0.2 copy-done.6
  7.0 0.0 copy-done.7
  7.0 0.0 copy-done.3
  7.0 0.0 copy-done.4
  7.0 0.0 copy-start.1
  7.0 1.6 copy-done.1
  8.6 0.0 copy-start.2
  8.6 1.6 copy-done.2
  10.2 11.0 %shard_map.121.kv_ref = bf16[4,2048,128]{2,1,0:T(8,128)(2,1)S(1)} custom-call(s32[8,16]{1,0:T(8,128)S(1)} %copy-done.3, s32[8,16]{1,0:T(8,128)S(1)} %copy-done.4, bf16[2048,512]{1,0:T(8,128)(2,1)S(1)} %copy-done.1, bf16[2048,256]{1,0:T(8,128)(2,1)S(1)} %get-tuple-element.14.k_ref, bf16[2048,256]{1,0:T(8,128)(2,1)S(1)} %get-tuple-element.13.v_ref, ...), custom_call_target="tpu_custom_call" | custom-call | tf_op jit(solution)/shard_map/pallas_call | solution.py:66
  21.2 0.0 copy-start
  21.2 1.3 copy-done
  22.5 0.0 copy-start.8
  22.5 162.9 %shard_map.122 = (f32[4,4,128,128]{3,2,1,0:T(8,128)}, f32[4,4,128]{2,1,0:T(4,128)}) custom-call(bf16[4,2048,128]{2,1,0:T(8,128)(2,1)} %copy-done, bf16[2048,1024]{1,0:T(8,128)(2,1)} %layer_ref.1), custom_call_target="tpu_custom_call" | custom-call | tf_op jit(solution)/shard_map/pallas_call | solution.py:295
  185.4 0.8 reduce_sum.9
  186.2 0.1 copy.20
  186.3 0.1 div.39
  186.4 0.0 copy-done.8
  186.4 0.6 sqrt_add_fusion
  187.0 0.1 broadcast_bitcast_fusion
  187.1 1.3 broadcast_multiply_fusion
  188.4 0.0 copy-start.5
  188.4 0.8 copy.19
  189.2 1.2 mul.31
  190.4 0.0 copy-done.5
  190.4 2.4 %multiply_divide_fusion = (f32[128,2,1024]{2,1,0:T(2,128)}, f32[128,2,1024]{2,1,0:T(2,128)}) fusion(f32[2,1024]{1,0:T(2,128)S(1)} %bitcast.20, f32[128,2,1024]{2,1,0:T(2,128)S(1)} %mul.31, f32[128,2,1024]{2,1,0:T(2,128)S(1)} %copy-done.5), kind=kLoop, calls=%fused_computation.2 | loop fusion | flops 1048576 | bytes 4202496 | tf_op jit(solution)/shard_map/div | solution.py:354
  (6 shorter events, 0.1 us)
Async XLA Ops:
  6.2 0.7 copy-start.6
  6.2 0.8 copy-start.7
  6.2 0.8 copy-start.3
  6.2 0.8 copy-start.4
  7.0 1.6 copy-start.1
  8.6 1.6 copy-start.2
  21.2 1.3 copy-start
  22.5 163.9 %copy-start.8 = (f32[2,8]{1,0:T(2,128)S(1)}, f32[2,8]{1,0:T(2,128)}, u32[]{:S(2)}) copy-start(f32[2,8]{1,0:T(2,128)} %param.19) | copy-start | bytes 196
  188.4 2.0 %copy-start.5 = (f32[128,2,1024]{2,1,0:T(2,128)S(1)}, f32[128,2,1024]{2,1,0:T(2,128)}, u32[]{:S(2)}) copy-start(f32[128,2,1024]{2,1,0:T(2,128)} %param.18) | copy-start | bytes 3145732
where the time goes:
time: 193 us
  Pallas kernels  174 us (90%)
  local copies, waits for them, and re-layouts  13.1 us (7%)
  other arithmetic  5.09 us (3%)
    pallas_call x1, Pallas kernels, sum_over_groups(): pl.pallas_call(functools.partial(sum_kernel, groups, planes, 1.0 / math.s...  163 us
    pallas_call x1, Pallas kernels, attend(): pl.pallas_call(functools.partial(attend_kernel, tiles, group_size), grid=...  11 us
    slice x1, local copies, waits for them, and re-layouts, per_device(): keys, values = (keys_values[:, 0], keys_values[:, 1])  5.55 us
    unnamed x20, local copies, waits for them, and re-layouts  4.83 us

commit v1 on v0

v1 whole, which is shorter than its diff:
```python
import functools
import math

import jax
import jax.numpy as jnp
from jax import lax
from jax.experimental import pallas as pl
from jax.experimental.pallas import tpu as pltpu
from jax.sharding import PartitionSpec as P

D = 4096
HD = 128

ADAM_ONE = 0.9
ADAM_TWO = 0.95
ADAM_EPS = 1e-08
MESH = pl.DeviceIdType.MESH
NT = (((1,), (1,)), ((), ()))


def attend_kernel(tiles, group_size, fill_ref, cont_ref, q_ref, k_ref, v_ref, do_ref, lse_ref, delta_ref, out_ref):
    group = lax.axis_index("dp")
    block = k_ref.shape[0] // tiles
    scale_qk = HD ** (-0.5)
    wide = 2 * group_size * block
    key_place = lax.broadcasted_iota(jnp.int32, (block, wide), 0)
    column = lax.broadcasted_iota(jnp.int32, (block, wide), 1)
    query_place = column % block
    is_next = column >= group_size * block

    def one_tile(tile, carry):
        after = jnp.minimum(tile + 1, tiles - 1)
        here = pl.ds(pl.multiple_of(tile * block, block), block)
        there = pl.ds(pl.multiple_of(after * block, block), block)
        fill_here = fill_ref[group, tile]
        fill_there = jnp.where(tile + 1 < tiles, fill_ref[group, after] * (cont_ref[group, after] == 1).astype(jnp.int32), 0)
        heads = [slice(h * HD, (h + 1) * HD) for h in range(group_size)]
        q_cat = jnp.concatenate([q_ref[w, h] for w in (here, there) for h in heads], 0)
        do_cat = jnp.concatenate([do_ref[w, h] for w in (here, there) for h in heads], 0)
        lse = jnp.concatenate([lse_ref[0, h : h + 1, w] for w in (here, there) for h in range(group_size)], 1)
        delta = jnp.concatenate([delta_ref[0, h : h + 1, w] for w in (here, there) for h in range(group_size)], 1)
        scores = lax.dot_general(k_ref[here, :], q_cat, NT, preferred_element_type=jnp.float32) * scale_qk
        limit = jnp.where(is_next, fill_there, fill_here)
        allowed = (query_place < limit) & (is_next | (query_place >= key_place))
        prob = jnp.where(allowed, jnp.exp(scores - lse), 0.0)
        dprob = lax.dot_general(v_ref[here, :], do_cat, NT, preferred_element_type=jnp.float32)
        dscore = prob * (dprob - delta)
        value_grad = jnp.dot(prob.astype(jnp.bfloat16), do_cat, preferred_element_type=jnp.float32)
        key_grad = jnp.dot(dscore.astype(jnp.bfloat16), q_cat, preferred_element_type=jnp.float32) * scale_qk
        out_ref[0, here, :] = key_grad.astype(jnp.bfloat16)
        out_ref[1, here, :] = value_grad.astype(jnp.bfloat16)
        return carry

    lax.fori_loop(0, tiles, one_tile, 0, unroll=2)


def attend(queries, keys, values, out_grads, lse_rows, delta_rows, tile_fill, tile_cont):
    tokens = queries.shape[0]
    kv_local = keys.shape[1] // HD
    group_size = queries.shape[1] // keys.shape[1]
    tiles = tile_fill.shape[1]
    smem = pl.BlockSpec(memory_space=pltpu.SMEM)
    q_spec = pl.BlockSpec((tokens, group_size * HD), lambda h: (0, h))
    k_spec = pl.BlockSpec((tokens, HD), lambda h: (0, h))
    row_spec = pl.BlockSpec((1, group_size, tokens), lambda h: (h, 0, 0))
    return pl.pallas_call(
        functools.partial(attend_kernel, tiles, group_size),
        grid=(kv_local,),
        out_shape=jax.ShapeDtypeStruct((2 * kv_local, tokens, HD), jnp.bfloat16),
        in_specs=[smem, smem, q_spec, k_spec, k_spec, q_spec, row_spec, row_spec],
        out_specs=pl.BlockSpec((2, tokens, HD), lambda h: (h, 0, 0)),
        compiler_params=pltpu.CompilerParams(vmem_limit_bytes=32 * 2**20),
    )(tile_fill, tile_cont, queries, keys, values, out_grads, lse_rows, delta_rows)


def token_split(tokens, planes):
    if planes < 4 or tokens < 1024:
        return tokens
    return tokens - tokens * 3 // 8 // 128 * 128


def sum_kernel(
    groups, planes, split, inv, kv_ref, layer_ref, out_ref, sq_ref,
    layer, flipped, gathered, lent, lent_flipped, keep, pair_send, pair_recv, chip_send, chip_recv,
    part_send, part_recv, squares, sq_all,
    load_sem, own_sem, kv_right, kv_left, kv_recv, lent_ssem, lent_rsem, pair_ssem, pair_rsem, chip_ssem, chip_rsem,
    part_ssem, part_rsem, sq_ssem, sq_rsem,
):
    me, plane = lax.axis_index("dp"), lax.axis_index("tensor")
    chips = groups // 2
    chip, core = me // 2, me % 2
    partner = me + 1 - 2 * core
    chunks, tokens, _ = kv_ref.shape
    rows = layer_ref.shape[1]
    rows_out = rows // groups
    half = rows // 2
    events = planes * chunks
    lending = split < tokens
    is_end = (plane == 0) | (plane == planes - 1)
    is_helper = (plane == 1) | (plane == planes - 2)
    helped = jnp.where(plane == 1, 0, planes - 1)
    helper = jnp.where(plane == 0, 1, planes - 2)
    mid = split // 256 * 128
    segments = ((split, tokens - split), (0, mid), (mid, split - mid)) if lending else ((0, mid), (mid, split - mid))

    load = pltpu.make_async_copy(layer_ref, layer, load_sem)
    load.start()
    own = [pltpu.make_async_copy(kv_ref.at[c], gathered.at[c, plane], own_sem.at[c]) for c in range(chunks)]
    for c in range(chunks):
        own[c].start()

    barrier = pltpu.get_barrier_semaphore()
    mine = me * planes + plane

    def greet(step, carry):
        other = lax.rem(mine + step, groups * planes)
        pl.semaphore_signal(barrier, inc=1, device_id=(other // planes, other % planes), device_id_type=MESH)
        return carry

    lax.fori_loop(1, groups * planes, greet, 0)
    pl.semaphore_wait(barrier, groups * planes - 1)

    far = jnp.where(plane < planes // 2, 1, -1)
    near_count = jnp.minimum(plane, planes - 1 - plane)

    def piece_of(w):
        turn = (w + 1) // 2
        swing = jnp.where(w % 2 == 1, turn, -turn)
        return plane + far * jnp.where(w <= 2 * near_count, swing, w - near_count)

    def turn_of(e):
        k = e - 2 * chunks
        last, odd = k == 2 * chunks - 1, k % 2 == 1
        mixed = (planes >= 4) & (k >= 0) & (k < 2 * chunks)
        w = jnp.where(last | (jnp.logical_not(odd) & (k > 0)), 3, 2)
        c = jnp.where(last, chunks - 1, jnp.where(odd, (k + 1) // 2, jnp.maximum(k // 2 - 1, 0)))
        return jnp.where(mixed, w, e // chunks), jnp.where(mixed, c, e % chunks)

    def place(e):
        w, c = turn_of(e)
        return c, piece_of(w)

    def lend_copy():
        return pltpu.make_async_remote_copy(
            src_ref=layer_ref.at[pl.ds(split, tokens - split), :], dst_ref=lent, send_sem=lent_ssem,
            recv_sem=lent_rsem, device_id=(me, helper), device_id_type=MESH,
        )

    def move(c, p, s, right):
        start, size = segments[s]
        where = gathered.at[c, p, pl.ds(start, size)]
        to = jnp.minimum(plane + 1, planes - 1) if right else jnp.maximum(plane - 1, 0)
        return pltpu.make_async_remote_copy(
            src_ref=where, dst_ref=where, send_sem=(kv_right if right else kv_left).at[c, p, s],
            recv_sem=kv_recv.at[c, p, s], device_id=(me, to), device_id_type=MESH,
        )

    def passes(p, s, right):
        lent_part = lending and s == 0
        if right:
            there = plane < planes - 2 if lent_part else plane < planes - 1
            return (p <= plane) & there
        there = plane > 1 if lent_part else plane > 0
        return (p >= plane) & there

    def pass_on(c, p, s):
        for right in (True, False):
            @pl.when(passes(p, s, right))
            def _():
                move(c, p, s, right).start()

    def arrive(c, p, s):
        if lending and s == 0:
            @pl.when(jnp.logical_not(is_end))
            def _():
                move(c, p, s, True).wait_recv()
        else:
            move(c, p, s, True).wait_recv()

    row_block = min(256, half)

    def multiply(source, lhs_from, rhs_from, length, c, p, job):
        weights = (c, p, pl.ds(rhs_from, length))

        def sent(i, carry):
            at = pl.multiple_of(i * row_block, row_block)
            pair_send[job, pl.ds(at, row_block), :] = jnp.dot(
                source[pl.ds(half + at, row_block), pl.ds(lhs_from, length)], gathered[weights],
                preferred_element_type=jnp.float32,
            ).astype(jnp.bfloat16)
            return carry

        def kept(i, carry):
            at = pl.multiple_of(i * row_block, row_block)
            keep[job, pl.ds(at, row_block), :] = jnp.dot(
                source[pl.ds(at, row_block), pl.ds(lhs_from, length)], gathered[weights],
                preferred_element_type=jnp.float32,
            )
            return carry

        lax.fori_loop(0, half // row_block, sent, 0)
        pair_copy(job).start()
        lax.fori_loop(0, half // row_block, kept, 0)

    def slice_of(k):
        return pl.ds(pl.multiple_of(k * rows_out, rows_out), rows_out)

    def pair_copy(job):
        return pltpu.make_async_remote_copy(
            src_ref=pair_send.at[job], dst_ref=pair_recv.at[job], send_sem=pair_ssem.at[job],
            recv_sem=pair_rsem.at[job], device_id=(partner, plane), device_id_type=MESH,
        )

    def chip_copy(job, step):
        other = lax.rem(chip + step, chips)
        return pltpu.make_async_remote_copy(
            src_ref=chip_send.at[job, step - 1], dst_ref=chip_recv.at[job, step - 1],
            send_sem=chip_ssem.at[job, step - 1], recv_sem=chip_rsem.at[job, step - 1],
            device_id=(2 * other + core, plane), device_id_type=MESH,
        )

    def part_copy(c, p):
        return pltpu.make_async_remote_copy(
            src_ref=part_send.at[c, p], dst_ref=part_recv.at[c, p], send_sem=part_ssem.at[c, p],
            recv_sem=part_rsem.at[c, p], device_id=(me, helped), device_id_type=MESH,
        )

    def own_job(c, p):
        return c * planes + p

    def part_job(c, p):
        return events + c * planes + p

    def scatter(job):
        pair_copy(job).wait_recv()
        for step in range(1, chips):
            other = slice_of(lax.rem(chip + step, chips))
            both = keep[job, other, :] + pair_recv[job, other, :].astype(jnp.float32)
            chip_send[job, step - 1] = both.astype(jnp.bfloat16)
            chip_copy(job, step).start()

    def total_of(job):
        mine = slice_of(chip)
        total = keep[job, mine, :] + pair_recv[job, mine, :].astype(jnp.float32)
        for step in range(1, chips):
            chip_copy(job, step).wait_recv()
            total = total + chip_recv[job, step - 1].astype(jnp.float32)
        return total

    def finish(c, p, total):
        total = total * inv
        out_ref[c, p] = total
        squares[pl.ds(c * planes + p, 1), :] = jnp.sum(total * total, axis=0, keepdims=True)

    def helped_total(c, p, total):
        part_copy(c, p).wait_recv()
        return total + part_recv[c, p].astype(jnp.float32)

    def gather_own(e):
        w, c = turn_of(e)
        p = piece_of(w)
        total = total_of(own_job(c, p))
        if not lending:
            finish(c, p, total)
            return
        plain = jnp.logical_not(is_end) | (w == 0)

        @pl.when(plain)
        def _():
            finish(c, p, total)

        @pl.when(is_end & (w >= 3))
        def _():
            finish(c, p, helped_total(c, p, total))

        @pl.when(is_end & ((w == 1) | (w == 2)))
        def _():
            out_ref[c, p] = total

    def late_finish(e):
        turn, c = turn_of(e)

        @pl.when(is_end & (turn == 3))
        def _():
            for w in (1, 2):
                p = piece_of(w)
                finish(c, p, helped_total(c, p, out_ref[c, p]))

    def for_parts(e, act):
        w, c = turn_of(e)

        @pl.when(is_helper & (w == 2))
        def _():
            def both(i, carry):
                act(c, piece_of(i))
                return carry

            lax.fori_loop(0, 2, both, 0)

        @pl.when(is_helper & (w >= 3))
        def _():
            act(c, piece_of(w))

    def part_multiply(c, p):
        multiply(lent_flipped, 0, split, tokens - split, c, p, part_job(c, p))

    def part_scatter(c, p):
        scatter(part_job(c, p))

    def part_gather(c, p):
        part_send[c, p] = total_of(part_job(c, p)).astype(jnp.bfloat16)
        part_copy(c, p).start()

    unit = min(128, rows_out)
    flip_block = 128

    def flip(source, target, i, carry):
        turned = source[:, pl.ds(pl.multiple_of(i * flip_block, flip_block), flip_block)].T
        for sub in range(flip_block // unit):
            start = i * flip_block + sub * unit
            piece = start // rows_out
            owner = piece // 2 + jnp.where(piece % 2 == core, 0, chips)
            to = pl.multiple_of(owner * rows_out + start % rows_out, unit)
            target[pl.ds(to, unit), :] = turned[sub * unit : (sub + 1) * unit]
        return carry

    if lending:
        @pl.when(is_end)
        def _():
            lend_copy().start()

    for c in range(chunks):
        own[c].wait()
        for s in range(len(segments)):
            pass_on(c, plane, s)

    load.wait()
    lax.fori_loop(0, rows // flip_block, functools.partial(flip, layer, flipped), 0)

    def one_event(e, carry):
        w, c = turn_of(e)
        p = piece_of(w)

        @pl.when(w > 0)
        def _():
            for s in range(len(segments)):
                arrive(c, p, s)
                pass_on(c, p, s)

        if lending:
            @pl.when(is_helper & (e == 2 * chunks))
            def _():
                lend_copy().wait_recv()
                lax.fori_loop(0, rows // flip_block, functools.partial(flip, lent, lent_flipped), 0)

            for_parts(e, part_multiply)
            short = is_end & (w > 0)

            @pl.when(short)
            def _():
                multiply(flipped, 0, 0, split, c, p, own_job(c, p))

            @pl.when(jnp.logical_not(short))
            def _():
                multiply(flipped, 0, 0, tokens, c, p, own_job(c, p))
        else:
            multiply(flipped, 0, 0, tokens, c, p, own_job(c, p))

        @pl.when(e >= 1)
        def _():
            if lending:
                for_parts(e - 1, part_scatter)
            scatter(own_job(*place(e - 1)))

        @pl.when(e >= 2)
        def _():
            if lending:
                for_parts(e - 2, part_gather)
            gather_own(e - 2)

        if lending:
            late_finish(e)
        return carry

    lax.fori_loop(0, events, one_event, 0)
    if lending:
        for_parts(events - 1, part_scatter)
    scatter(own_job(*place(events - 1)))
    if lending:
        for_parts(events - 2, part_gather)
        for_parts(events - 1, part_gather)
    gather_own(events - 2)
    gather_own(events - 1)

    lane_sums = jnp.sum(squares[...], axis=1, keepdims=True)
    row = lax.broadcasted_iota(jnp.int32, (squares.shape[0], HD), 0)
    lane = lax.broadcasted_iota(jnp.int32, (squares.shape[0], HD), 1)
    sq_all[mine] = jnp.sum(jnp.where(row == lane, lane_sums, 0.0), axis=0, keepdims=True)

    def sq_copy(step):
        other = lax.rem(mine + step, groups * planes)
        return pltpu.make_async_remote_copy(
            src_ref=sq_all.at[mine], dst_ref=sq_all.at[mine], send_sem=sq_ssem, recv_sem=sq_rsem,
            device_id=(other // planes, other % planes), device_id_type=MESH,
        )

    def send_squares(step, carry):
        sq_copy(step).start()
        return carry

    lax.fori_loop(1, groups * planes, send_squares, 0)
    others = sq_all.at[pl.ds(0, groups * planes - 1)]
    pltpu.make_async_copy(others, others, sq_rsem).wait()
    sq_ref[...] = jnp.sum(sq_all[...], axis=0)
    pltpu.make_async_copy(others, others, sq_ssem).wait()

    if lending:
        @pl.when(is_end)
        def _():
            lend_copy().wait_send()

    def drain_job(job):
        pair_copy(job).wait_send()
        for step in range(1, chips):
            chip_copy(job, step).wait_send()

    def drain(e, carry):
        c, p = e // planes, e % planes
        drain_job(own_job(c, p))
        if lending:
            @pl.when(is_helper & (p != helped))
            def _():
                drain_job(part_job(c, p))
                part_copy(c, p).wait_send()

        for s in range(len(segments)):
            for right in (True, False):
                @pl.when(passes(p, s, right))
                def _():
                    move(c, p, s, right).wait_send()
        return carry

    lax.fori_loop(0, events, drain, 0)


def sum_over_groups(kv_chunks, layer_input, groups, planes):
    chunks, tokens, _ = kv_chunks.shape
    rows = layer_input.shape[1]
    rows_out = rows // groups
    chips = groups // 2
    split = token_split(tokens, planes)
    lent = max(tokens - split, 128)
    jobs = (2 if split < tokens else 1) * chunks * planes
    segments = 3 if split < tokens else 2
    half, full = jnp.bfloat16, jnp.float32
    dma = pltpu.SemaphoreType.DMA
    vmem = pl.BlockSpec(memory_space=pltpu.VMEM)
    anywhere = pl.BlockSpec(memory_space=pl.ANY)
    return pl.pallas_call(
        functools.partial(sum_kernel, groups, planes, split, 1.0 / math.sqrt(tokens * groups)),
        out_shape=(
            jax.ShapeDtypeStruct((chunks, planes, rows_out, HD), full),
            jax.ShapeDtypeStruct((1, HD), full),
        ),
        in_specs=[anywhere, anywhere],
        out_specs=(vmem, vmem),
        scratch_shapes=[
            pltpu.VMEM((tokens, rows), half),
            pltpu.VMEM((rows, tokens), half),
            pltpu.VMEM((chunks, planes, tokens, HD), half),
            pltpu.VMEM((lent, rows), half),
            pltpu.VMEM((rows, lent), half),
            pltpu.VMEM((jobs, rows // 2, HD), full),
            pltpu.VMEM((jobs, rows // 2, HD), half),
            pltpu.VMEM((jobs, rows // 2, HD), half),
            pltpu.VMEM((jobs, chips - 1, rows_out, HD), half),
            pltpu.VMEM((jobs, chips - 1, rows_out, HD), half),
            pltpu.VMEM((chunks, planes, rows_out, HD), half),
            pltpu.VMEM((chunks, planes, rows_out, HD), half),
            pltpu.VMEM((chunks * planes, HD), full),
            pltpu.VMEM((groups * planes, 1, HD), full),
            dma,
            dma((chunks,)),
            dma((chunks, planes, segments)),
            dma((chunks, planes, segments)),
            dma((chunks, planes, segments)),
            dma,
            dma,
            dma((jobs,)),
            dma((jobs,)),
            dma((jobs, chips - 1)),
            dma((jobs, chips - 1)),
            dma((chunks, planes)),
            dma((chunks, planes)),
            dma,
            dma,
        ],
        compiler_params=pltpu.CompilerParams(
            collective_id=0, has_side_effects=True, vmem_limit_bytes=56 * 2**20
        ),
    )(kv_chunks, layer_input)


def per_device(
    layer_input, queries, keys_values, out_grads, log_sums, deltas, tile_fill, tile_cont, moment_first, moment_second
):
    groups, planes = lax.axis_size("dp"), lax.axis_size("tensor")
    keys, values = keys_values[:, 0], keys_values[:, 1]
    tokens = queries.shape[0]
    kv_local = keys.shape[1] // HD
    lse_rows = log_sums.astype(jnp.float32).T.reshape(kv_local, -1, tokens)
    delta_rows = deltas.astype(jnp.float32).T.reshape(kv_local, -1, tokens)
    kv_chunks = attend(queries, keys, values, out_grads, lse_rows, delta_rows, tile_fill, tile_cont)
    summed, square_row = sum_over_groups(kv_chunks, layer_input, groups, planes)
    rows_out = summed.shape[2]
    heads_kv = moment_second.shape[1]
    parts = summed.reshape(kv_local, 2, planes, rows_out, HD)
    proj_grads = parts.transpose(3, 1, 2, 0, 4).reshape(rows_out, 2, -1)
    squares = square_row[0, : 2 * heads_kv].reshape(kv_local, 2, planes).transpose(1, 2, 0).reshape(2, heads_kv)
    new_first = ADAM_ONE * moment_first + (1 - ADAM_ONE) * proj_grads
    new_second = ADAM_TWO * moment_second + (1 - ADAM_TWO) * squares / (D * HD)
    step_size = jnp.sqrt(new_second / (1 - ADAM_TWO**2)) + ADAM_EPS
    scaled = (new_first / (1 - ADAM_ONE**2)).reshape(rows_out, 2, heads_kv, -1)
    update = (scaled / step_size[None, :, :, None]).reshape(proj_grads.shape)
    return (update, new_first, new_second)


def solution(mesh):
    in_specs = (
        P("dp", "tensor"),
        P("dp", "tensor"),
        P("dp", None, "tensor"),
        P("dp", "tensor"),
        P("dp", "tensor"),
        P("dp", "tensor"),
        P(),
        P(),
        P(("tensor", "dp"), None, None),
        P(),
    )
    out_specs = (P(("tensor", "dp"), None, None), P(("tensor", "dp"), None, None), P())
    return jax.shard_map(
        per_device, mesh=mesh, in_specs=in_specs, out_specs=out_specs, check_vma=False
    )
```

time: 193 us -> 156 us (0.81)
  Pallas kernels: 174 us -> 137 us
    pallas_call x1, Pallas kernels: 163 us -> 126 us  [sum_over_groups(): pl.pallas_call(functools.partial(sum_kernel, groups, planes, split, 1.0 /...]
where the time goes in v1:
time: 156 us
  Pallas kernels  137 us (88%)
  local copies, waits for them, and re-layouts  13.2 us (8%)
  other arithmetic  4.98 us (3%)
    pallas_call x1, Pallas kernels, sum_over_groups(): pl.pallas_call(functools.partial(sum_kernel, groups, planes, split, 1.0 /...  126 us
    pallas_call x1, Pallas kernels, attend(): pl.pallas_call(functools.partial(attend_kernel, tiles, group_size), grid=...  11 us
    slice x1, local copies, waits for them, and re-layouts, per_device(): keys, values = (keys_values[:, 0], keys_values[:, 1])  5.55 us
    unnamed x20, local copies, waits for them, and re-layouts  4.83 us

profile of v1, /device:TPU:0, one launch (start us, length us, event | category | flops | bytes accessed | tf_op | source)
XLA Modules:
  0.0 155.8 jit_solution(12127587509352283761)
XLA Ops:
  0.6 5.6 %fusion = (bf16[2048,1,256]{2,1,0:T(2,128)(2,1)S(1)}, bf16[2048,1,256]{2,1,0:T(2,128)(2,1)S(1)}) fusion(bf16[2048,2,256]{2,1,0:T(2,128)(2,1)} %param.12), kind=kLoop, calls=%fused_computation.12 | loop fusion | bytes 4194304 | tf_op jit(solution)/shard_map/slice | solution.py:508
  6.2 0.0 copy-start.6
  6.2 0.0 copy-start.7
  6.2 0.0 copy-start.3
  6.2 0.0 copy-start.4
  6.2 0.5 copy_bitcast_fusion
  6.7 0.2 copy-done.6
  7.0 0.0 copy-done.7
  7.0 0.0 copy-done.3
  7.0 0.0 copy-done.4
  7.0 0.0 copy-start.1
  7.0 1.6 %copy-done.1 = bf16[2048,512]{1,0:T(8,128)(2,1)S(1)} copy-done((bf16[2048,512]{1,0:T(8,128)(2,1)S(1)}, bf16[2048,512]{1,0:T(8,128)(2,1)}, u32[]{:S(2)}) %copy-start.1) | copy-done | bytes 2097176
  8.6 0.0 copy-start.2
  8.6 1.6 %copy-done.2 = bf16[2048,512]{1,0:T(8,128)(2,1)S(1)} copy-done((bf16[2048,512]{1,0:T(8,128)(2,1)S(1)}, bf16[2048,512]{1,0:T(8,128)(2,1)}, u32[]{:S(2)}) %copy-start.2) | copy-done | bytes 2097176
  10.2 11.0 %shard_map.121.kv_ref = bf16[4,2048,128]{2,1,0:T(8,128)(2,1)S(1)} custom-call(s32[8,16]{1,0:T(8,128)S(1)} %copy-done.3, s32[8,16]{1,0:T(8,128)S(1)} %copy-done.4, bf16[2048,512]{1,0:T(8,128)(2,1)S(1)} %copy-done.1, bf16[2048,256]{1,0:T(8,128)(2,1)S(1)} %get-tuple-element.14.k_ref, bf16[2048,256]{1,0:T(8,128)(2,1)S(1)} %get-tuple-element.13.v_ref, ...), custom_call_target="tpu_custom_call" | custom-call | tf_op jit(solution)/shard_map/pallas_call | solution.py:66
  21.2 0.0 copy-start
  21.2 1.3 copy-done
  22.5 0.0 copy-start.8
  22.5 125.8 %shard_map.122 = (f32[4,4,128,128]{3,2,1,0:T(8,128)}, f32[1,128]{1,0:T(1,128)}) custom-call(bf16[4,2048,128]{2,1,0:T(8,128)(2,1)} %copy-done, bf16[2048,1024]{1,0:T(8,128)(2,1)} %layer_ref.1), custom_call_target="tpu_custom_call" | custom-call | tf_op jit(solution)/shard_map/pallas_call | solution.py:459
  148.4 0.7 multiply_reduce_fusion
  149.1 0.1 div.37
  149.2 0.1 copy.20
  149.3 0.1 div.39
  149.3 0.0 copy-done.8
  149.3 0.6 sqrt_add_fusion
  149.9 0.1 broadcast_bitcast_fusion
  150.0 1.3 broadcast_multiply_fusion
  151.3 0.0 copy-start.5
  151.3 0.8 copy.19
  152.1 1.2 mul.31
  153.4 0.0 copy-done.5
  153.4 2.4 %multiply_divide_fusion = (f32[128,2,1024]{2,1,0:T(2,128)}, f32[128,2,1024]{2,1,0:T(2,128)}) fusion(f32[2,1024]{1,0:T(2,128)S(1)} %bitcast.18, f32[128,2,1024]{2,1,0:T(2,128)S(1)} %mul.31, f32[128,2,1024]{2,1,0:T(2,128)S(1)} %copy-done.5), kind=kLoop, calls=%fused_computation.2 | loop fusion | flops 1048576 | bytes 4202496 | tf_op jit(solution)/shard_map/div | solution.py:524
  (5 shorter events, 0.1 us)
Async XLA Ops:
  6.2 0.7 copy-start.6
  6.2 0.8 copy-start.7
  6.2 0.8 copy-start.3
  6.2 0.8 copy-start.4
  7.0 1.6 %copy-start.1 = (bf16[2048,512]{1,0:T(8,128)(2,1)S(1)}, bf16[2048,512]{1,0:T(8,128)(2,1)}, u32[]{:S(2)}) copy-start(bf16[2048,512]{1,0:T(8,128)(2,1)} %q_ref.1) | copy-start | bytes 6291460
  8.6 1.6 %copy-start.2 = (bf16[2048,512]{1,0:T(8,128)(2,1)S(1)}, bf16[2048,512]{1,0:T(8,128)(2,1)}, u32[]{:S(2)}) copy-start(bf16[2048,512]{1,0:T(8,128)(2,1)} %do_ref.1) | copy-start | bytes 6291460
  21.2 1.3 copy-start
  22.5 126.8 %copy-start.8 = (f32[2,8]{1,0:T(2,128)S(1)}, f32[2,8]{1,0:T(2,128)}, u32[]{:S(2)}) copy-start(f32[2,8]{1,0:T(2,128)} %param.19) | copy-start | bytes 196
  151.3 2.0 %copy-start.5 = (f32[128,2,1024]{2,1,0:T(2,128)S(1)}, f32[128,2,1024]{2,1,0:T(2,128)}, u32[]{:S(2)}) copy-start(f32[128,2,1024]{2,1,0:T(2,128)} %param.18) | copy-start | bytes 3145732

commit v2 on v1

--- a/solution.py
+++ b/solution.py
@@ -10,6 +10,7 @@
 
 D = 4096
 HD = 128
+GRAIN = 16
 
 ADAM_ONE = 0.9
 ADAM_TWO = 0.95
@@ -18,9 +19,10 @@
 NT = (((1,), (1,)), ((), ()))
 
 
-def attend_kernel(tiles, group_size, fill_ref, cont_ref, q_ref, k_ref, v_ref, do_ref, lse_ref, delta_ref, out_ref):
+def attend_tiles(tiles, group_size, fill_ref, cont_ref, q_ref, kv_ref, do_ref, lse_ref, delta_ref, key_out, value_out):
     group = lax.axis_index("dp")
-    block = k_ref.shape[0] // tiles
+    tokens, _, local = kv_ref.shape
+    block = tokens // tiles
     scale_qk = HD ** (-0.5)
     wide = 2 * group_size * block
     key_place = lax.broadcasted_iota(jnp.int32, (block, wide), 0)
@@ -28,60 +30,61 @@
     query_place = column % block
     is_next = column >= group_size * block
 
-    def one_tile(tile, carry):
+    def one_tile(h, tile):
         after = jnp.minimum(tile + 1, tiles - 1)
         here = pl.ds(pl.multiple_of(tile * block, block), block)
         there = pl.ds(pl.multiple_of(after * block, block), block)
         fill_here = fill_ref[group, tile]
         fill_there = jnp.where(tile + 1 < tiles, fill_ref[group, after] * (cont_ref[group, after] == 1).astype(jnp.int32), 0)
-        heads = [slice(h * HD, (h + 1) * HD) for h in range(group_size)]
-        q_cat = jnp.concatenate([q_ref[w, h] for w in (here, there) for h in heads], 0)
-        do_cat = jnp.concatenate([do_ref[w, h] for w in (here, there) for h in heads], 0)
-        lse = jnp.concatenate([lse_ref[0, h : h + 1, w] for w in (here, there) for h in range(group_size)], 1)
-        delta = jnp.concatenate([delta_ref[0, h : h + 1, w] for w in (here, there) for h in range(group_size)], 1)
-        scores = lax.dot_general(k_ref[here, :], q_cat, NT, preferred_element_type=jnp.float32) * scale_qk
+        heads = [slice((h * group_size + j) * HD, (h * group_size + j + 1) * HD) for j in range(group_size)]
+        q_cat = jnp.concatenate([q_ref[w, j] for w in (here, there) for j in heads], 0)
+        do_cat = jnp.concatenate([do_ref[w, j] for w in (here, there) for j in heads], 0)
+        lse = jnp.concatenate([lse_ref[h, j : j + 1, w] for w in (here, there) for j in range(group_size)], 1)
+        delta = jnp.concatenate([delta_ref[h, j : j + 1, w] for w in (here, there) for j in range(group_size)], 1)
+        pairs = kv_ref[here].reshape(block, 2 * local)
+        keys, values = pairs[:, h * HD : (h + 1) * HD], pairs[:, local + h * HD : local + (h + 1) * HD]
+        scores = lax.dot_general(keys, q_cat, NT, preferred_element_type=jnp.float32) * scale_qk
         limit = jnp.where(is_next, fill_there, fill_here)
         allowed = (query_place < limit) & (is_next | (query_place >= key_place))
         prob = jnp.where(allowed, jnp.exp(scores - lse), 0.0)
-        dprob = lax.dot_general(v_ref[here, :], do_cat, NT, preferred_element_type=jnp.float32)
+        dprob = lax.dot_general(values, do_cat, NT, preferred_element_type=jnp.float32)
         dscore = prob * (dprob - delta)
         value_grad = jnp.dot(prob.astype(jnp.bfloat16), do_cat, preferred_element_type=jnp.float32)
         key_grad = jnp.dot(dscore.astype(jnp.bfloat16), q_cat, preferred_element_type=jnp.float32) * scale_qk
-        out_ref[0, here, :] = key_grad.astype(jnp.bfloat16)
-        out_ref[1, here, :] = value_grad.astype(jnp.bfloat16)
-        return carry
-
-    lax.fori_loop(0, tiles, one_tile, 0, unroll=2)
-
-
-def attend(queries, keys, values, out_grads, lse_rows, delta_rows, tile_fill, tile_cont):
-    tokens = queries.shape[0]
-    kv_local = keys.shape[1] // HD
-    group_size = queries.shape[1] // keys.shape[1]
-    tiles = tile_fill.shape[1]
-    smem = pl.BlockSpec(memory_space=pltpu.SMEM)
-    q_spec = pl.BlockSpec((tokens, group_size * HD), lambda h: (0, h))
-    k_spec = pl.BlockSpec((tokens, HD), lambda h: (0, h))
-    row_spec = pl.BlockSpec((1, group_size, tokens), lambda h: (h, 0, 0))
-    return pl.pallas_call(
-        functools.partial(attend_kernel, tiles, group_size),
-        grid=(kv_local,),
-        out_shape=jax.ShapeDtypeStruct((2 * kv_local, tokens, HD), jnp.bfloat16),
-        in_specs=[smem, smem, q_spec, k_spec, k_spec, q_spec, row_spec, row_spec],
-        out_specs=pl.BlockSpec((2, tokens, HD), lambda h: (h, 0, 0)),
-        compiler_params=pltpu.CompilerParams(vmem_limit_bytes=32 * 2**20),
-    )(tile_fill, tile_cont, queries, keys, values, out_grads, lse_rows, delta_rows)
+        key_out(h, here, key_grad.astype(jnp.bfloat16))
+        value_out(h, here, value_grad.astype(jnp.bfloat16))
+
+    return one_tile
 
 
 def token_split(tokens, planes):
     if planes < 4 or tokens < 1024:
         return tokens
-    return tokens - tokens * 3 // 8 // 128 * 128
+    return tokens - tokens * 5 // 16 // 128 * 128
+
+
+def capacities(tokens):
+    if tokens < 1024:
+        return [tokens]
+    return [tokens * part // 16 // 128 * 128 for part in (12, 13, 14)] + [tokens]
+
+
+def find_sources(tile_fill, positions):
+    tiles = tile_fill.shape[1]
+    live = (tile_fill + GRAIN - 1) // GRAIN
+    upto = jnp.arange(tiles)[:, None] >= jnp.arange(tiles)[None, :]
+    ends = jnp.sum(jnp.where(upto[None], live[:, None, :], 0), axis=2)
+    group = jnp.arange(positions // GRAIN)
+    passed = group[None, :, None] >= ends[:, None, :]
+    skipped = positions // tiles // GRAIN - live
+    source = group[None, :] + jnp.sum(jnp.where(passed, skipped[:, None, :], 0), axis=2)
+    return jnp.minimum(source, positions // GRAIN), jnp.max(jnp.sum(live, axis=1)) * GRAIN
 
 
 def sum_kernel(
-    groups, planes, split, inv, kv_ref, layer_ref, out_ref, sq_ref,
-    layer, flipped, gathered, lent, lent_flipped, keep, pair_send, pair_recv, chip_send, chip_recv,
+    groups, planes, tiles, split, inv,
+    fill_ref, cont_ref, source_ref, q_hbm, kv_hbm, do_hbm, lse_ref, delta_ref, layer_ref, out_ref, sq_ref,
+    q_ref, kv_ref, do_ref, raw, packed, layer, flipped, gathered, lent, lent_flipped, keep, pair_send, pair_recv, chip_send, chip_recv,
     part_send, part_recv, squares, sq_all,
     load_sem, own_sem, kv_right, kv_left, kv_recv, lent_ssem, lent_rsem, pair_ssem, pair_rsem, chip_ssem, chip_rsem,
     part_ssem, part_rsem, sq_ssem, sq_rsem,
@@ -90,8 +93,10 @@
     chips = groups // 2
     chip, core = me // 2, me % 2
     partner = me + 1 - 2 * core
-    chunks, tokens, _ = kv_ref.shape
-    rows = layer_ref.shape[1]
+    chunks, _, tokens, _ = gathered.shape
+    positions = q_ref.shape[0]
+    packing = tokens < positions
+    rows = layer_ref.shape[-1]
     rows_out = rows // groups
     half = rows // 2
     events = planes * chunks
@@ -100,14 +105,18 @@
     is_helper = (plane == 1) | (plane == planes - 2)
     helped = jnp.where(plane == 1, 0, planes - 1)
     helper = jnp.where(plane == 0, 1, planes - 2)
-    mid = split // 256 * 128
+    mid = split // 2 // (positions // tiles) * (positions // tiles)
     segments = ((split, tokens - split), (0, mid), (mid, split - mid)) if lending else ((0, mid), (mid, split - mid))
 
-    load = pltpu.make_async_copy(layer_ref, layer, load_sem)
-    load.start()
-    own = [pltpu.make_async_copy(kv_ref.at[c], gathered.at[c, plane], own_sem.at[c]) for c in range(chunks)]
-    for c in range(chunks):
-        own[c].start()
+    loads = [
+        pltpu.make_async_copy(source, target, own_sem.at[i])
+        for i, (source, target) in enumerate(((kv_hbm, kv_ref), (q_hbm, q_ref), (do_hbm, do_ref)))
+    ]
+    for load in loads:
+        load.start()
+    rows_held = layer.at[pl.ds(0, positions // GRAIN)] if packing else layer
+    layer_load = pltpu.make_async_copy(layer_ref, rows_held, load_sem)
+    layer_load.start()
 
     barrier = pltpu.get_barrier_semaphore()
     mine = me * planes + plane
@@ -142,7 +151,7 @@
 
     def lend_copy():
         return pltpu.make_async_remote_copy(
-            src_ref=layer_ref.at[pl.ds(split, tokens - split), :], dst_ref=lent, send_sem=lent_ssem,
+            src_ref=(packed if packing else layer_ref).at[pl.ds(split, tokens - split), :], dst_ref=lent, send_sem=lent_ssem,
             recv_sem=lent_rsem, device_id=(me, helper), device_id_type=MESH,
         )
 
@@ -324,18 +333,76 @@
             target[pl.ds(to, unit), :] = turned[sub * unit : (sub + 1) * unit]
         return carry
 
+    block = positions // tiles
+    def pack_layer(start, size):
+        def one(g, carry):
+            to = pl.multiple_of(g * GRAIN, GRAIN)
+            packed[pl.ds(to, GRAIN), :] = layer[source_ref[me, g]]
+            return carry
+
+        lax.fori_loop(start // GRAIN, (start + size) // GRAIN, one, 0, unroll=4)
+
+    def pack_own(h, start, size):
+        def one(g, carry):
+            to = pl.multiple_of(g * GRAIN, GRAIN)
+            for c in (2 * h, 2 * h + 1):
+                gathered[c, plane, pl.ds(to, GRAIN), :] = raw[c, source_ref[me, g]]
+            return carry
+
+        lax.fori_loop(start // GRAIN, (start + size) // GRAIN, one, 0, unroll=4)
+
+    if packing:
+        for c in range(chunks):
+            raw[c, positions // GRAIN] = jnp.zeros((GRAIN, HD), jnp.bfloat16)
+        layer[positions // GRAIN] = jnp.zeros(layer.shape[1:], jnp.bfloat16)
+        layer_load.wait()
+        pack_layer(split, tokens - split)
     if lending:
         @pl.when(is_end)
         def _():
             lend_copy().start()
 
-    for c in range(chunks):
-        own[c].wait()
-        for s in range(len(segments)):
-            pass_on(c, plane, s)
-
-    load.wait()
-    lax.fori_loop(0, rows // flip_block, functools.partial(flip, layer, flipped), 0)
+    for load in loads:
+        load.wait()
+
+    def put(offset):
+        def store(h, where, value):
+            if packing:
+                groups_of = pl.ds(where.start // GRAIN, where.size // GRAIN)
+                raw[2 * h + offset, groups_of] = value.reshape(where.size // GRAIN, GRAIN, HD)
+            else:
+                gathered[2 * h + offset, plane, where, :] = value
+
+        return store
+
+    group_size = q_ref.shape[1] // (chunks // 2 * HD)
+    one_tile = attend_tiles(
+        tiles, group_size, fill_ref, cont_ref, q_ref, kv_ref, do_ref, lse_ref, delta_ref, put(0), put(1)
+    )
+
+    def attend(h, first, last):
+        def tile_step(tile, carry):
+            one_tile(h, tile)
+            return carry
+
+        lax.fori_loop(first, last, tile_step, 0)
+
+    for h in range(chunks // 2):
+        if packing:
+            attend(h, 0, tiles)
+        for s, (start, size) in enumerate(segments):
+            if packing:
+                pack_own(h, start, size)
+            else:
+                attend(h, start // block, (start + size) // block)
+            for c in (2 * h, 2 * h + 1):
+                pass_on(c, plane, s)
+
+    if packing:
+        pack_layer(0, split)
+    else:
+        layer_load.wait()
+    lax.fori_loop(0, rows // flip_block, functools.partial(flip, packed if packing else layer, flipped), 0)
 
     def one_event(e, carry):
         w, c = turn_of(e)
@@ -443,11 +510,18 @@
     lax.fori_loop(0, events, drain, 0)
 
 
-def sum_over_groups(kv_chunks, layer_input, groups, planes):
-    chunks, tokens, _ = kv_chunks.shape
+def sum_over_groups(
+    tile_fill, tile_cont, sources, queries, keys_values, out_grads, lse_rows, delta_rows, layer_input, groups, planes, number, tokens
+):
+    positions, _, local = keys_values.shape
+    chunks = 2 * (local // HD)
+    tiles = tile_fill.shape[1]
     rows = layer_input.shape[1]
+    if tokens < positions:
+        layer_input = layer_input.reshape(positions // GRAIN, GRAIN, rows)
     rows_out = rows // groups
     chips = groups // 2
+    packing = tokens < positions
     split = token_split(tokens, planes)
     lent = max(tokens - split, 128)
     jobs = (2 if split < tokens else 1) * chunks * planes
@@ -456,16 +530,22 @@
     dma = pltpu.SemaphoreType.DMA
     vmem = pl.BlockSpec(memory_space=pltpu.VMEM)
     anywhere = pl.BlockSpec(memory_space=pl.ANY)
+    smem = pl.BlockSpec(memory_space=pltpu.SMEM)
     return pl.pallas_call(
-        functools.partial(sum_kernel, groups, planes, split, 1.0 / math.sqrt(tokens * groups)),
+        functools.partial(sum_kernel, groups, planes, tiles, split, 1.0 / math.sqrt(positions * groups)),
         out_shape=(
             jax.ShapeDtypeStruct((chunks, planes, rows_out, HD), full),
             jax.ShapeDtypeStruct((1, HD), full),
         ),
-        in_specs=[anywhere, anywhere],
+        in_specs=[smem, smem, smem, anywhere, anywhere, anywhere, vmem, vmem, anywhere],
         out_specs=(vmem, vmem),
         scratch_shapes=[
-            pltpu.VMEM((tokens, rows), half),
+            pltpu.VMEM(queries.shape, half),
+            pltpu.VMEM(keys_values.shape, half),
+            pltpu.VMEM(out_grads.shape, half),
+            pltpu.VMEM((chunks, positions // GRAIN + 1, GRAIN, HD) if packing else (GRAIN, HD), half),
+            pltpu.VMEM((tokens, rows) if packing else (GRAIN, HD), half),
+            pltpu.VMEM((positions // GRAIN + 1, GRAIN, rows) if packing else (positions, rows), half),
             pltpu.VMEM((rows, tokens), half),
             pltpu.VMEM((chunks, planes, tokens, HD), half),
             pltpu.VMEM((lent, rows), half),
@@ -480,7 +560,7 @@
             pltpu.VMEM((chunks * planes, HD), full),
             pltpu.VMEM((groups * planes, 1, HD), full),
             dma,
-            dma((chunks,)),
+            dma((3,)),
             dma((chunks, planes, segments)),
             dma((chunks, planes, segments)),
             dma((chunks, planes, segments)),
@@ -496,22 +576,29 @@
             dma,
         ],
         compiler_params=pltpu.CompilerParams(
-            collective_id=0, has_side_effects=True, vmem_limit_bytes=56 * 2**20
+            collective_id=number, has_side_effects=True, vmem_limit_bytes=60 * 2**20
         ),
-    )(kv_chunks, layer_input)
+    )(tile_fill, tile_cont, sources, queries, keys_values, out_grads, lse_rows, delta_rows, layer_input)
 
 
 def per_device(
     layer_input, queries, keys_values, out_grads, log_sums, deltas, tile_fill, tile_cont, moment_first, moment_second
 ):
     groups, planes = lax.axis_size("dp"), lax.axis_size("tensor")
-    keys, values = keys_values[:, 0], keys_values[:, 1]
     tokens = queries.shape[0]
-    kv_local = keys.shape[1] // HD
+    kv_local = keys_values.shape[2] // HD
     lse_rows = log_sums.astype(jnp.float32).T.reshape(kv_local, -1, tokens)
     delta_rows = deltas.astype(jnp.float32).T.reshape(kv_local, -1, tokens)
-    kv_chunks = attend(queries, keys, values, out_grads, lse_rows, delta_rows, tile_fill, tile_cont)
-    summed, square_row = sum_over_groups(kv_chunks, layer_input, groups, planes)
+    lengths = capacities(tokens)
+    sources, needed = find_sources(tile_fill, tokens)
+    summed, square_row = lax.switch(
+        sum((needed > length).astype(jnp.int32) for length in lengths[:-1]) if len(lengths) > 1 else 0,
+        [
+            functools.partial(sum_over_groups, groups=groups, planes=planes, number=i, tokens=length)
+            for i, length in enumerate(lengths)
+        ],
+        tile_fill, tile_cont, sources, queries, keys_values, out_grads, lse_rows, delta_rows, layer_input,
+    )
     rows_out = summed.shape[2]
     heads_kv = moment_second.shape[1]
     parts = summed.reshape(kv_local, 2, planes, rows_out, HD)

time: 156 us -> 126 us (0.81)
  Pallas kernels: 137 us -> 115 us
  local copies, waits for them, and re-layouts: 13.2 us -> 2.44 us
    pallas_call x2 -> x1, Pallas kernels: 137 us -> 115 us  [sum_over_groups(): pl.pallas_call(functools.partial(sum_kernel, groups, planes, tiles, split...]
    slice x1 -> x0, local copies, waits for them, and re-layouts: 5.55 us -> none  [per_device(): keys, values = (keys_values[:, 0], keys_values[:, 1])]
    unnamed x20 -> x6, local copies, waits for them, and re-layouts: 4.83 us -> 0.09 us
where the time goes in v2:
time: 126 us; the launch traced here: 125 us
  Pallas kernels  115 us (91%)
  other arithmetic  6.32 us (5%)
  local copies, waits for them, and re-layouts  2.44 us (2%)
  between operations  1.38 us (1%)
    pallas_call x1, Pallas kernels, sum_over_groups(): pl.pallas_call(functools.partial(sum_kernel, groups, planes, tiles, split...  115 us

profile of v2, /device:TPU:0, one launch (start us, length us, event | category | flops | bytes accessed | tf_op | source)
XLA Modules:
  0.0 125.2 jit_solution(9993871443445492507)
XLA Ops:
  0.6 0.7 broadcast_subtract_fusion
  1.3 0.1 reduce_sum.27
  1.5 0.6 reduce_max.9
  2.8 0.2 select_reduce_fusion.1
  3.0 0.1 select_reduce_fusion
  3.1 0.7 convert_bitcast_fusion.1
  3.9 0.7 convert_bitcast_fusion
  4.6 115.1 %conditional.1 = (f32[4,4,128,128]{3,2,1,0:T(8,128)S(1)}, f32[1,16]{1,0:T(1,128)S(1)}) conditional(s32[]{:T(128)} %clamp.3, (bf16[2048,1024]{1,0:T(8,128)(2,1)}, s32[8,16]{1,0:T(8,128)}, s32[8,16]{1,0:T(8,128)}, s32[8,128]{1,0:T(8,128)S(1)}, bf16[2048,512]{1,0:T(8,128)(2,1)}, ...), branch_computations={%region_4.5_spmd, %region_5.6_spmd, %region_6.7_spmd, %region_7.8_... | conditional | bytes 16 | solution.py:594
  4.7 114.8 %branch_1_fun.1 = (f32[4,4,128,128]{3,2,1,0:T(8,128)S(1)}, f32[1,128]{1,0:T(1,128)S(1)}) custom-call(s32[8,16]{1,0:T(8,128)} %get-tuple-element.81.fill_ref, s32[8,16]{1,0:T(8,128)} %get-tuple-element.82.cont_ref, s32[8,128]{1,0:T(8,128)S(1)} %get-tuple-element.83.source_ref, bf16[2048,512]{1,0:T(8,128)(2,1)} %get-tuple-element.84.q_hbm, ...), custom_call_target="tpu_custom_call" | custom-call | tf_op jit(solution)/shard_map/cond/branch_1_fun/pallas_call | solution.py:534
  119.7 0.1 broadcast_multiply_fusion
  119.8 0.0 copy-start.1
  119.8 0.0 copy-start
  119.8 0.8 copy.22
  120.7 1.2 mul.35
  121.9 0.1 div.53
  122.0 0.1 copy.18
  122.1 0.1 div.55
  122.2 0.0 copy-done.1
  122.2 0.6 sqrt_add_fusion
  122.7 0.1 broadcast_bitcast_fusion
  122.8 0.0 copy-done
  122.8 2.4 %multiply_divide_fusion = (f32[128,2,1024]{2,1,0:T(2,128)}, f32[128,2,1024]{2,1,0:T(2,128)}) fusion(f32[2,1024]{1,0:T(2,128)S(1)} %bitcast.26, f32[128,2,1024]{2,1,0:T(2,128)S(1)} %mul.35, f32[128,2,1024]{2,1,0:T(2,128)S(1)} %copy-done), kind=kLoop, calls=%fused_computation.1 | loop fusion | flops 1048576 | bytes 4202496 | tf_op jit(solution)/shard_map/div | solution.py:611
  (6 shorter events, 0.1 us)
Async XLA Ops:
  119.8 2.3 %copy-start.1 = (f32[2,8]{1,0:T(2,128)S(1)}, f32[2,8]{1,0:T(2,128)}, u32[]{:S(2)}) copy-start(f32[2,8]{1,0:T(2,128)} %param.23) | copy-start | bytes 196
  119.8 3.0 %copy-start = (f32[128,2,1024]{2,1,0:T(2,128)S(1)}, f32[128,2,1024]{2,1,0:T(2,128)}, u32[]{:S(2)}) copy-start(f32[128,2,1024]{2,1,0:T(2,128)} %param.22) | copy-start | bytes 3145732

commit v3 on v2

--- a/solution.py
+++ b/solution.py
@@ -39,8 +39,8 @@
         heads = [slice((h * group_size + j) * HD, (h * group_size + j + 1) * HD) for j in range(group_size)]
         q_cat = jnp.concatenate([q_ref[w, j] for w in (here, there) for j in heads], 0)
         do_cat = jnp.concatenate([do_ref[w, j] for w in (here, there) for j in heads], 0)
-        lse = jnp.concatenate([lse_ref[h, j : j + 1, w] for w in (here, there) for j in range(group_size)], 1)
-        delta = jnp.concatenate([delta_ref[h, j : j + 1, w] for w in (here, there) for j in range(group_size)], 1)
+        lse = jnp.concatenate([lse_ref[h * group_size + j : h * group_size + j + 1, w] for w in (here, there) for j in range(group_size)], 1)
+        delta = jnp.concatenate([delta_ref[h * group_size + j : h * group_size + j + 1, w] for w in (here, there) for j in range(group_size)], 1)
         pairs = kv_ref[here].reshape(block, 2 * local)
         keys, values = pairs[:, h * HD : (h + 1) * HD], pairs[:, local + h * HD : local + (h + 1) * HD]
         scores = lax.dot_general(keys, q_cat, NT, preferred_element_type=jnp.float32) * scale_qk
@@ -83,8 +83,8 @@
 
 def sum_kernel(
     groups, planes, tiles, split, inv,
-    fill_ref, cont_ref, source_ref, q_hbm, kv_hbm, do_hbm, lse_ref, delta_ref, layer_ref, out_ref, sq_ref,
-    q_ref, kv_ref, do_ref, raw, packed, layer, flipped, gathered, lent, lent_flipped, keep, pair_send, pair_recv, chip_send, chip_recv,
+    fill_ref, cont_ref, source_ref, q_hbm, kv_hbm, do_hbm, lse_half, delta_half, layer_ref, out_ref, sq_ref,
+    q_ref, kv_ref, do_ref, lse_ref, delta_ref, raw, packed, layer, flipped, gathered, lent, lent_flipped, keep, pair_send, pair_recv, chip_send, chip_recv,
     part_send, part_recv, squares, sq_all,
     load_sem, own_sem, kv_right, kv_left, kv_recv, lent_ssem, lent_rsem, pair_ssem, pair_rsem, chip_ssem, chip_rsem,
     part_ssem, part_rsem, sq_ssem, sq_rsem,
@@ -362,6 +362,8 @@
         def _():
             lend_copy().start()
 
+    lse_ref[...] = lse_half[...].astype(jnp.float32)
+    delta_ref[...] = delta_half[...].astype(jnp.float32)
     for load in loads:
         load.wait()
 
@@ -385,7 +387,7 @@
             one_tile(h, tile)
             return carry
 
-        lax.fori_loop(first, last, tile_step, 0)
+        lax.fori_loop(first, last, tile_step, 0, unroll=2 if packing else 1)
 
     for h in range(chunks // 2):
         if packing:
@@ -543,6 +545,8 @@
             pltpu.VMEM(queries.shape, half),
             pltpu.VMEM(keys_values.shape, half),
             pltpu.VMEM(out_grads.shape, half),
+            pltpu.VMEM(lse_rows.shape, full),
+            pltpu.VMEM(delta_rows.shape, full),
             pltpu.VMEM((chunks, positions // GRAIN + 1, GRAIN, HD) if packing else (GRAIN, HD), half),
             pltpu.VMEM((tokens, rows) if packing else (GRAIN, HD), half),
             pltpu.VMEM((positions // GRAIN + 1, GRAIN, rows) if packing else (positions, rows), half),
@@ -587,8 +591,7 @@
     groups, planes = lax.axis_size("dp"), lax.axis_size("tensor")
     tokens = queries.shape[0]
     kv_local = keys_values.shape[2] // HD
-    lse_rows = log_sums.astype(jnp.float32).T.reshape(kv_local, -1, tokens)
-    delta_rows = deltas.astype(jnp.float32).T.reshape(kv_local, -1, tokens)
+    lse_rows, delta_rows = log_sums.T, deltas.T
     lengths = capacities(tokens)
     sources, needed = find_sources(tile_fill, tokens)
     summed, square_row = lax.switch(

time: 126 us -> 123 us (0.976)
  other arithmetic: 6.32 us -> 4.87 us
    reshape x2 -> x0, other arithmetic: 1.45 us -> none  [the longest x1 0.73 us: per_device(): lse_rows = log_sums.astype(jnp.float32).T.reshape(kv_local, -1, tokens)]
    pallas_call x1, Pallas kernels: 115 us -> 114 us  [sum_over_groups(): pl.pallas_call(functools.partial(sum_kernel, groups, planes, tiles, split...]
where the time goes in v3:
time: 123 us; the launch traced here: 122 us
  Pallas kernels  114 us (93%)
  other arithmetic  4.87 us (4%)
  local copies, waits for them, and re-layouts  2.37 us (2%)
  between operations  1.37 us (1%)
    pallas_call x1, Pallas kernels, sum_over_groups(): pl.pallas_call(functools.partial(sum_kernel, groups, planes, tiles, split...  114 us

profile of v3, /device:TPU:0, one launch (start us, length us, event | category | flops | bytes accessed | tf_op | source)
XLA Modules:
  0.0 122.4 jit_solution(12312104701190731225)
XLA Ops:
  0.6 0.7 broadcast_subtract_fusion
  1.3 0.1 reduce_sum.27
  1.5 0.6 reduce_max.9
  2.8 0.2 select_reduce_fusion.1
  3.0 0.1 select_reduce_fusion
  3.1 113.8 %conditional.1 = (f32[4,4,128,128]{3,2,1,0:T(8,128)S(1)}, f32[1,16]{1,0:T(1,128)S(1)}) conditional(s32[]{:T(128)} %clamp.3, (bf16[2048,1024]{1,0:T(8,128)(2,1)}, s32[8,16]{1,0:T(8,128)}, s32[8,16]{1,0:T(8,128)}, s32[8,128]{1,0:T(8,128)S(1)}, bf16[2048,512]{1,0:T(8,128)(2,1)}, ...), branch_computations={%region_4.5_spmd, %region_5.6_spmd, %region_6.7_spmd, %region_7.8_... | conditional | bytes 16 | solution.py:597
  3.1 113.5 %branch_1_fun.1 = (f32[4,4,128,128]{3,2,1,0:T(8,128)S(1)}, f32[1,128]{1,0:T(1,128)S(1)}) custom-call(s32[8,16]{1,0:T(8,128)} %get-tuple-element.81.fill_ref, s32[8,16]{1,0:T(8,128)} %get-tuple-element.82.cont_ref, s32[8,128]{1,0:T(8,128)S(1)} %get-tuple-element.83.source_ref, bf16[2048,512]{1,0:T(8,128)(2,1)} %get-tuple-element.84.q_hbm, ...), custom_call_target="tpu_custom_call" | custom-call | tf_op jit(solution)/shard_map/cond/branch_1_fun/pallas_call | solution.py:536
  116.9 0.1 broadcast_multiply_fusion
  117.0 0.0 copy-start.1
  117.0 0.0 copy-start
  117.0 0.8 copy.22
  117.9 1.2 mul.35
  119.1 0.1 div.53
  119.2 0.1 copy.18
  119.3 0.1 div.55
  119.4 0.0 copy-done.1
  119.4 0.6 sqrt_add_fusion
  119.9 0.1 broadcast_bitcast_fusion
  120.0 0.0 copy-done
  120.0 2.4 %multiply_divide_fusion = (f32[128,2,1024]{2,1,0:T(2,128)}, f32[128,2,1024]{2,1,0:T(2,128)}) fusion(f32[2,1024]{1,0:T(2,128)S(1)} %bitcast.32, f32[128,2,1024]{2,1,0:T(2,128)S(1)} %mul.35, f32[128,2,1024]{2,1,0:T(2,128)S(1)} %copy-done), kind=kLoop, calls=%fused_computation.1 | loop fusion | flops 1048576 | bytes 4202496 | tf_op jit(solution)/shard_map/div | solution.py:614
  (4 shorter events, 0.0 us)
Async XLA Ops:
  117.0 2.3 %copy-start.1 = (f32[2,8]{1,0:T(2,128)S(1)}, f32[2,8]{1,0:T(2,128)}, u32[]{:S(2)}) copy-start(f32[2,8]{1,0:T(2,128)} %param.23) | copy-start | bytes 196
  117.0 3.0 %copy-start = (f32[128,2,1024]{2,1,0:T(2,128)S(1)}, f32[128,2,1024]{2,1,0:T(2,128)}, u32[]{:S(2)}) copy-start(f32[128,2,1024]{2,1,0:T(2,128)} %param.22) | copy-start | bytes 3145732
